TPU v7x, 32 devices: a whole 2x2x4 slice. The times are simulated.
32 devices in a mesh: row: 4 (over y, x), col: 8 (over z, core).
Axes of the slice: x: 2, y: 2, z: 4, core: 2. Of those that a mesh axis runs over, the one named last changes fastest.
Arguments:
- tiles: bfloat16 [4, 8, 128, 128, 128], P('row', 'col'), may hold values from 0 to 0.31
- block_rows: int32 [4, 8, 128], P('row', 'col'), may hold values from 0 to 63, as said below
- block_cols: int32 [4, 8, 128], P('row', 'col'), may hold values from 0 to 127
- counts: int32 [4, 8], P('row', 'col'), may hold values from 1 to 128, as said below
- seeds: int32 [8, 65536], P(None, ('col', 'row')), may hold values from 1 to 999
Outputs:
- vectors_out: float32 [8, 65536], P(None, ('col', 'row'))
- deltas: float32 [4, 8], replicated
Inputs may be any that keep to these rules, and one draw needn't show every extreme that they name: `counts`: each entry is 1, a half, a quarter or an eighth of 128 (at least 1); some device is full in every draw. On each device, among the values of block_rows (over all 128 slots) that share one quotient by 16, at most 4 are distinct; on a device whose count is 128, some quotient has exactly 4 distinct values among its tiles.
All inputs are finite; a program needn't handle non-finite values.
Results may differ from a plain program's by a relative error of at most 0.00061.
Values may be sent and summed in bfloat16 or wider, within the bound.
A program may use at most 64 MiB of HBM per device.

v0:
```python
import jax
import jax.numpy as jnp
from jax import lax
from jax.sharding import PartitionSpec as P

BLOCK = 128
TILE_BLOCK = 32
ITERS = 4
ROW_CAP = 4


def apply_tiles(partial_value, gathered, panel_block, target_block, cols_block, weight):
    taken_rows = gathered[cols_block]
    product = jnp.einsum(
        "tkc,trc->tkr", taken_rows, panel_block, preferred_element_type=jnp.float32
    )
    return partial_value.at[target_block].add(product * weight[:, None, None])


def on_device(tiles, block_rows, block_cols, counts, seeds):
    panels = tiles[0, 0]
    rows_local = block_rows[0, 0]
    cols_local = block_cols[0, 0]
    count_here = counts[0, 0]
    vectors = seeds.shape[0]
    piece_len = seeds.shape[1]
    piece_blocks = piece_len // BLOCK
    row_count = lax.axis_size("row")
    total_nodes = piece_len * row_count * lax.axis_size("col")
    row_span = row_count * piece_blocks
    tile_total = panels.shape[0]
    lane_index = jnp.arange(TILE_BLOCK, dtype=jnp.int32)
    tile_index = jnp.arange(tile_total, dtype=jnp.int32)
    live_flag = tile_index < count_here
    live_mask = live_flag.astype(jnp.float32)
    block_index = jnp.arange(row_span, dtype=jnp.int32)
    hits = (rows_local[None, :] == block_index[:, None]) & live_flag[None, :]
    present = jnp.max(hits.astype(jnp.int32), axis=1).reshape(row_count, piece_blocks)
    rank = jnp.cumsum(present, axis=1) - present
    owner_index = jnp.arange(row_count, dtype=jnp.int32)
    block_slot = (owner_index[:, None] * ROW_CAP + rank).reshape(row_span)
    slot_total = row_count * ROW_CAP
    matched = jnp.where(rows_local[:, None] == block_index[None, :], block_slot[None, :], 0)
    targets = jnp.minimum(jnp.sum(matched, axis=1), slot_total - 1)
    slot_index = jnp.arange(ROW_CAP, dtype=jnp.int32)
    offset_index = jnp.arange(piece_blocks, dtype=jnp.int32)
    matches = (present[:, None, :] == 1) & (rank[:, None, :] == slot_index[None, :, None])
    slot_ids = jnp.sum(jnp.where(matches, offset_index[None, None, :], 0), axis=2)
    row_total = jnp.sum(panels, axis=2, dtype=jnp.float32) * live_mask[:, None]
    degree_part = (
        jnp.zeros((slot_total, 1, BLOCK), jnp.float32).at[targets].add(row_total[:, None, :])
    )
    seed_float = seeds.astype(jnp.float32)
    seed_total = lax.psum(jnp.sum(seed_float, axis=1), ("row", "col"))
    current = (
        (total_nodes * seed_float / seed_total[:, None])
        .reshape(vectors, piece_blocks, BLOCK)
        .transpose(1, 0, 2)
    )
    empty_sum = jnp.zeros((slot_total, vectors, BLOCK), jnp.float32)
    deltas = []
    divisor = None
    owner_table = None
    for iteration in range(ITERS):
        current_half = current.astype(jnp.bfloat16)
        gathered = lax.all_gather(current_half, "col", axis=0, tiled=True)

        def advance(block_at, partial_value):
            begin_at = block_at * TILE_BLOCK
            weight = (begin_at + lane_index < count_here).astype(jnp.float32)
            return apply_tiles(
                partial_value,
                gathered,
                lax.dynamic_slice_in_dim(panels, begin_at, TILE_BLOCK, 0),
                lax.dynamic_slice_in_dim(targets, begin_at, TILE_BLOCK, 0),
                lax.dynamic_slice_in_dim(cols_local, begin_at, TILE_BLOCK, 0),
                weight,
            )

        partial_value = lax.fori_loop(
            0, (count_here + TILE_BLOCK - 1) // TILE_BLOCK, advance, empty_sum
        )
        shaped = partial_value.reshape(row_count, ROW_CAP, vectors, BLOCK)
        if iteration == 0:
            degree_shaped = degree_part.reshape(row_count, ROW_CAP, 1, BLOCK)
            incoming, degree_in, received_ids = (
                lax.all_to_all(shaped, "row", split_axis=0, concat_axis=0, tiled=True),
                lax.all_to_all(degree_shaped, "row", split_axis=0, concat_axis=0, tiled=True),
                lax.all_to_all(slot_ids, "row", split_axis=0, concat_axis=0, tiled=True),
            )
            block_index_own = jnp.arange(piece_blocks, dtype=jnp.int32)
            owner_table = (received_ids.reshape(-1)[None, :] == block_index_own[:, None]).astype(
                jnp.float32
            )
            degree_piece = jnp.dot(
                owner_table,
                degree_in.reshape(row_count * ROW_CAP, BLOCK),
                precision=lax.Precision.HIGHEST,
                preferred_element_type=jnp.float32,
            )
            divisor = 1.0 + degree_piece.reshape(piece_blocks, 1, BLOCK)
        else:
            incoming = lax.all_to_all(shaped, "row", split_axis=0, concat_axis=0, tiled=True)
        summed = jnp.dot(
            owner_table,
            incoming.reshape(row_count * ROW_CAP, vectors * BLOCK),
            precision=lax.Precision.HIGHEST,
            preferred_element_type=jnp.float32,
        ).reshape(piece_blocks, vectors, BLOCK)
        raw_next = (summed + current) / divisor
        local_total = jnp.sum(raw_next, axis=(0, 2))
        totals = lax.psum(local_total, ("row", "col"))
        updated = total_nodes * raw_next / totals[None, :, None]
        deltas.append(lax.pmax(jnp.max(jnp.abs(updated - current), axis=(0, 2)), ("row", "col")))
        current = updated
    vectors_out = current.transpose(1, 0, 2).reshape(vectors, piece_len)
    return (vectors_out, jnp.stack(deltas))


def solution(mesh):
    placed = (
        P("row", "col", None, None, None),
        P("row", "col", None),
        P("row", "col", None),
        P("row", "col"),
        P(None, ("col", "row")),
    )
    return jax.shard_map(
        on_device,
        mesh=mesh,
        in_specs=placed,
        out_specs=(P(None, ("col", "row")), P()),
        check_vma=False,
    )
```

profile of v0, /device:TPU:0, one launch (start us, length us, event | category | flops | bytes accessed | tf_op | source)
XLA Modules:
  0.0 454.9 jit_solution(6785953493534906902)
XLA Ops:
  3.1 5.2 %all-to-all-start = ((s32[4,1,4]{2,1,0:T(1,128)}), s32[4,1,4]{2,1,0:T(1,128)S(1)}, u32[]{:S(2)}, u32[]{:S(2)}) async-start(s32[4,1,4]{2,1,0:T(1,128)} %bitcast.3), calls=%async_computation | async-start | bytes 4096 | tf_op jit(solution)/shard_map/all_to_all | solution.py:89
  10.3 40.9 %psum.35 = f32[8]{0:T(128)S(1)} all-reduce(f32[8]{0:T(128)S(1)} %convert_reduce_fusion.1), channel_id=1, replica_groups=mesh['row'=4,'col'=8] {'row','col'}, use_global_device_ids=true, to_apply=%region_5.6 | all-reduce | flops 8 | bytes 64 | tf_op jit(solution)/shard_map/psum | solution.py:54
  52.2 14.3 %all_gather.12 = bf16[128,8,128]{2,0,1:T(8,128)(2,1)S(1)} all-gather(bf16[16,8,128]{2,0,1:T(8,128)(2,1)S(1)} %bitcast.214), channel_id=1, replica_groups=mesh['row'=4,'col'=8] {'col'}, dimensions={0}, use_global_device_ids=true | all-gather | bytes 294912 | tf_op jit(solution)/shard_map/all_gather | solution.py:66
  75.8 28.4 %while.44 = (s32[]{:T(128)}, f32[16,8,128]{2,1,0:T(8,128)}, s32[]{:T(128)}, s32[128]{0:T(128)S(1)}, s32[128]{0:T(128)S(1)}, /*index=5*/bf16[128,8,128]{2,1,0:T(8...) while((s32[]{:T(128)}, f32[16,8,128]{2,1,0:T(8,128)}, ...), condition=%wide.region_8.9_spmd.clone, body=%wide.region_6.8_spmd.clone.sunk | while | flops 8455462 | bytes 1774899 | solution.py:80
  100.3 3.9 scatter_fusion
  108.9 4.7 %all-to-all-done.1 = f32[4,4,8,128]{3,2,1,0:T(8,128)S(1)} async-done(((f32[4,4,8,128]{3,2,1,0:T(8,128)}), f32[4,4,8,128]{3,2,1,0:T(8,128)S(1)}, u32[]{:S(2)}, u32[]{:S(2)}) %all-to-all-start.1) | async-done | bytes 65568 | tf_op jit(solution)/shard_map/all_to_all | solution.py:87
  113.9 38.4 %psum.36 = f32[8]{0:T(128)S(1)} all-reduce(f32[8]{0:T(128)S(1)} %get-tuple-element.490), channel_id=1, replica_groups=mesh['row'=4,'col'=8] {'row','col'}, use_global_device_ids=true, to_apply=%region_12.13 | all-reduce | flops 8 | bytes 64 | tf_op jit(solution)/shard_map/psum | solution.py:112
  152.3 14.2 %all_gather.13 = bf16[128,8,128]{2,0,1:T(8,128)(2,1)S(1)} all-gather(bf16[16,8,128]{2,0,1:T(8,128)(2,1)S(1)} %get-tuple-element.480), channel_id=1, replica_groups=mesh['row'=4,'col'=8] {'col'}, dimensions={0}, use_global_device_ids=true | all-gather | bytes 294912 | tf_op jit(solution)/shard_map/all_gather | solution.py:66
  167.3 28.4 %while.45 = (s32[]{:T(128)}, f32[16,8,128]{2,1,0:T(8,128)}, s32[]{:T(128)}, s32[128]{0:T(128)S(1)}, s32[128]{0:T(128)S(1)}, /*index=5*/bf16[128,8,128]{2,1,0:T(8...) while((s32[]{:T(128)}, f32[16,8,128]{2,1,0:T(8,128)}, ...), condition=%wide.region_15.16_spmd.clone, body=%wide.region_13.15_spmd.clone.sunk | while | flops 8455462 | bytes 1774899 | solution.py:80
  177.6 3.9 scatter_fusion.1
  191.8 3.9 scatter_fusion.1
  199.2 4.8 %all-to-all-done.3 = f32[4,4,8,128]{3,2,1,0:T(8,128)S(1)} async-done(((f32[4,4,8,128]{3,2,1,0:T(8,128)}), f32[4,4,8,128]{3,2,1,0:T(8,128)S(1)}, u32[]{:S(2)}, u32[]{:S(2)}) %all-to-all-start.3) | async-done | bytes 65568 | tf_op jit(solution)/shard_map/all_to_all | solution.py:103
  204.4 37.9 %psum.37 = f32[8]{0:T(128)S(1)} all-reduce(f32[8]{0:T(128)S(1)} %get-tuple-element.403), channel_id=1, replica_groups=mesh['row'=4,'col'=8] {'row','col'}, use_global_device_ids=true, to_apply=%region_17.18 | all-reduce | flops 8 | bytes 64 | tf_op jit(solution)/shard_map/psum | solution.py:112
  242.3 14.2 %all_gather.14 = bf16[128,8,128]{2,0,1:T(8,128)(2,1)S(1)} all-gather(bf16[16,8,128]{2,0,1:T(8,128)(2,1)S(1)} %get-tuple-element.478), channel_id=1, replica_groups=mesh['row'=4,'col'=8] {'col'}, dimensions={0}, use_global_device_ids=true | all-gather | bytes 294912 | tf_op jit(solution)/shard_map/all_gather | solution.py:66
  257.3 28.4 %while.46 = (s32[]{:T(128)}, f32[16,8,128]{2,1,0:T(8,128)}, s32[]{:T(128)}, s32[128]{0:T(128)S(1)}, s32[128]{0:T(128)S(1)}, /*index=5*/bf16[128,8,128]{2,1,0:T(8...) while((s32[]{:T(128)}, f32[16,8,128]{2,1,0:T(8,128)}, ...), condition=%wide.region_20.21_spmd.clone, body=%wide.region_18.20_spmd.clone.sunk | while | flops 8455462 | bytes 1774899 | solution.py:80
  267.6 3.9 scatter_fusion.2
  281.8 3.9 scatter_fusion.2
  289.3 4.8 %all-to-all-done.4 = f32[4,4,8,128]{3,2,1,0:T(8,128)S(1)} async-done(((f32[4,4,8,128]{3,2,1,0:T(8,128)}), f32[4,4,8,128]{3,2,1,0:T(8,128)S(1)}, u32[]{:S(2)}, u32[]{:S(2)}) %all-to-all-start.4) | async-done | bytes 65568 | tf_op jit(solution)/shard_map/all_to_all | solution.py:103
  294.4 37.7 %psum.38 = f32[8]{0:T(128)S(1)} all-reduce(f32[8]{0:T(128)S(1)} %get-tuple-element.405), channel_id=1, replica_groups=mesh['row'=4,'col'=8] {'row','col'}, use_global_device_ids=true, to_apply=%region_22.23 | all-reduce | flops 8 | bytes 64 | tf_op jit(solution)/shard_map/psum | solution.py:112
  332.1 14.5 %all_gather.15 = bf16[128,8,128]{2,0,1:T(8,128)(2,1)S(1)} all-gather(bf16[16,8,128]{2,0,1:T(8,128)(2,1)S(1)} %get-tuple-element.476), channel_id=1, replica_groups=mesh['row'=4,'col'=8] {'col'}, dimensions={0}, use_global_device_ids=true | all-gather | bytes 294912 | tf_op jit(solution)/shard_map/all_gather | solution.py:66
  346.8 19.7 %while.47 = (s32[]{:T(128)}, f32[16,8,128]{2,1,0:T(8,128)S(1)}, s32[]{:T(128)}, s32[128]{0:T(128)S(1)}, s32[128]{0:T(128)S(1)}, /*index=5*/bf16[128,8,128]{2,1,0...) while((s32[]{:T(128)}, f32[16,8,128]{2,1,0:T(8,128)S(1)}, ...), condition=%wide.region_25.26_spmd.clone, body=%wide.region_23.25_spmd.clone.sunk | while | flops 8455462 | bytes 1774899 | solution.py:80
  366.5 8.2 %all_to_all.34 = f32[4,4,8,128]{3,2,1,0:T(8,128)S(1)} all-to-all(f32[4,4,8,128]{3,2,1,0:T(8,128)S(1)} %bitcast.212), channel_id=1, replica_groups=mesh['row'=4,'col'=8] {'row'}, dimensions={0} | all-to-all | bytes 131072 | tf_op jit(solution)/shard_map/all_to_all | solution.py:103
  375.0 37.6 %psum.39 = f32[8]{0:T(128)S(1)} all-reduce(f32[8]{0:T(128)S(1)} %get-tuple-element.494), channel_id=1, replica_groups=mesh['row'=4,'col'=8] {'row','col'}, use_global_device_ids=true, to_apply=%region_27.28 | all-reduce | flops 8 | bytes 64 | tf_op jit(solution)/shard_map/psum | solution.py:112
  413.6 40.7 %all-reduce = (f32[1,8]{1,0:T(1,128)S(1)}, f32[1,8]{1,0:T(1,128)S(1)}, f32[1,8]{1,0:T(1,128)S(1)}, f32[1,8]{1,0:T(1,128)S(1)}) all-reduce(f32[1,8]{1,0:T(1,128)S(1)} %bitcast.222, f32[1,8]{1,0:T(1,128)S(1)} %bitcast.221, f32[1,8]{1,0:T(1,128)S(1)} %bitcast.224, f32[1,8]{1,0:T(1,128)S(1)} %bitcast.223), channel_id=1, replica_groups=mesh['row'=4,'col'=8] {'row','col'}, use_global_device_ids=true, to_apply=%region_35.36 | all-reduce | flops 32 | bytes 256 | tf_op jit(solution)/shard_map/pmax | solution.py:114
  (142 shorter events, 115.5 us)
Async XLA Ops:
  0.6 75.2 %copy-start = (s32[1,1,128]{2,1,0:T(1,128)S(1)}, s32[1,1,128]{2,1,0:T(1,128)}, u32[]{:S(2)}) copy-start(s32[1,1,128]{2,1,0:T(1,128)} %param.15) | copy-start | bytes 1540
  3.1 68.5 %all-to-all-start = ((s32[4,1,4]{2,1,0:T(1,128)}), s32[4,1,4]{2,1,0:T(1,128)S(1)}, u32[]{:S(2)}, u32[]{:S(2)}) async-start(s32[4,1,4]{2,1,0:T(1,128)} %bitcast.3), calls=%async_computation | async-start | bytes 4096 | tf_op jit(solution)/shard_map/all_to_all | solution.py:89
  71.6 33.8 %all-to-all-start.2 = ((f32[4,4,1,128]{3,1,2,0:T(4,128)}), f32[4,4,1,128]{3,1,2,0:T(4,128)S(1)}, u32[]{:S(2)}, u32[]{:S(2)}) async-start(f32[4,4,1,128]{3,1,2,0:T(4,128)} %bitcast.14), calls=%async_computation.2 | async-start | bytes 16384 | tf_op jit(solution)/shard_map/all_to_all | solution.py:88
  105.5 8.1 %all-to-all-start.1 = ((f32[4,4,8,128]{3,2,1,0:T(8,128)}), f32[4,4,8,128]{3,2,1,0:T(8,128)S(1)}, u32[]{:S(2)}, u32[]{:S(2)}) async-start(f32[4,4,8,128]{3,2,1,0:T(8,128)} %bitcast.8), calls=%async_computation.1 | async-start | bytes 131072 | tf_op jit(solution)/shard_map/all_to_all | solution.py:87
  195.7 8.4 %all-to-all-start.3 = ((f32[4,4,8,128]{3,2,1,0:T(8,128)}), f32[4,4,8,128]{3,2,1,0:T(8,128)S(1)}, u32[]{:S(2)}, u32[]{:S(2)}) async-start(f32[4,4,8,128]{3,2,1,0:T(8,128)} %bitcast.16), calls=%async_computation.3 | async-start | bytes 131072 | tf_op jit(solution)/shard_map/all_to_all | solution.py:103
  285.7 8.4 %all-to-all-start.4 = ((f32[4,4,8,128]{3,2,1,0:T(8,128)}), f32[4,4,8,128]{3,2,1,0:T(8,128)S(1)}, u32[]{:S(2)}, u32[]{:S(2)}) async-start(f32[4,4,8,128]{3,2,1,0:T(8,128)} %bitcast.18), calls=%async_computation.4 | async-start | bytes 131072 | tf_op jit(solution)/shard_map/all_to_all | solution.py:103
where the time goes:
time: 458 us; the launch traced here: 455 us
  blocking collectives  298 us (65%)
  other arithmetic  76.5 us (17%)
  matrix products  31 us (7%)
  starting transfers between devices  19.1 us (4%)
  waiting for transfers between devices  14.4 us (3%)
  local copies, waits for them, and re-layouts  13.7 us (3%)
    psum x4, blocking collectives, on_device(): totals = lax.psum(local_total, ('row', 'col'))  152 us
    all_gather x4, blocking collectives, on_device(): gathered = lax.all_gather(current_half, 'col', axis=0, tiled=True)  57.1 us
    scatter-add x16, other arithmetic, apply_tiles(): return partial_value.at[target_block].add(product * weight[:, None, None])  53.6 us
    psum x1, blocking collectives, on_device(): seed_total = lax.psum(jnp.sum(seed_float, axis=1), ('row', 'col'))  40.9 us
    pmax x1, blocking collectives, on_device(): lax.pmax(jnp.max(jnp.abs(updated - current), axis=(0, 2)), ('row', 'col'))  40.7 us
    dot_general x16, matrix products, apply_tiles(): jnp.einsum('tkc,trc->tkr', taken_rows, panel_block, preferred_element_typ...  29.7 us
    all_to_all x3, waiting for transfers between devices, on_device(): lax.all_to_all(shaped, 'row', split_axis=0, concat_axis=0, tiled=True)  14.4 us
    convert_element_type x16, other arithmetic, advance(): weight = (begin_at + lane_index < count_here).astype(jnp.float32)  10.4 us
  transfers between devices with their start and end apart: 5, of which 3 were waited for; matrix products, arithmetic and copies ran while one was open for 8% of the time, Pallas kernels for 0%

commit v1 on v0

--- a/solution.py
+++ b/solution.py
@@ -63,7 +63,14 @@
     owner_table = None
     for iteration in range(ITERS):
         current_half = current.astype(jnp.bfloat16)
-        gathered = lax.all_gather(current_half, "col", axis=0, tiled=True)
+        ring = [current_half]
+        for hop in range(7):
+            ring.append(lax.ppermute(ring[-1], "col", [(dev, (dev + 1) % 8) for dev in range(8)]))
+        gathered = jnp.roll(
+            jnp.concatenate(ring[::-1], axis=0),
+            (lax.axis_index("col") + 1) * ring[0].shape[0],
+            axis=0,
+        )
 
         def advance(block_at, partial_value):
             begin_at = block_at * TILE_BLOCK

time: 458 us -> 508 us (1.11)
  waiting for transfers between devices: 14.4 us -> 133 us
  blocking collectives: 298 us -> 256 us
  other arithmetic: 76.5 us -> 58.8 us
  starting transfers between devices: 19.1 us -> 12.7 us
    ppermute x0 -> x28, waiting for transfers between devices: none -> 128 us  [on_device(): lax.ppermute(ring[-1], 'col', [(dev, (dev + 1) % 8) for dev in range(8)])]
    all_gather x4 -> x0, blocking collectives: 57.1 us -> none  [on_device(): gathered = lax.all_gather(current_half, 'col', axis=0, tiled=True)]
    scatter-add x16, other arithmetic: 53.6 us -> 35.8 us  [apply_tiles(): return partial_value.at[target_block].add(product * weight[:, None, None])]
    all_to_all x1 -> x3, blocking collectives: 8.19 us -> 24.6 us  [on_device(): lax.all_to_all(shaped, 'row', split_axis=0, concat_axis=0, tiled=True)]
    all_to_all x3 -> x1, waiting for transfers between devices: 14.4 us -> 4.71 us  [on_device(): lax.all_to_all(shaped, 'row', split_axis=0, concat_axis=0, tiled=True)]
    all_to_all x3 -> x1, starting transfers between devices: 10.3 us -> 3.29 us  [on_device(): lax.all_to_all(shaped, 'row', split_axis=0, concat_axis=0, tiled=True)]
  transfers between devices with their start and end apart: 5 -> 31, of which waited for: 3 -> 27; matrix products, arithmetic and copies ran while one was open for 8% -> 7% of each run, Pallas kernels for 0% -> 0%
where the time goes in v1:
time: 508 us; the launch traced here: 506 us
  blocking collectives  256 us (50%)
  waiting for transfers between devices  133 us (26%)
  other arithmetic  58.8 us (12%)
  matrix products  31 us (6%)
  local copies, waits for them, and re-layouts  12.8 us (3%)
  starting transfers between devices  12.7 us (2%)
    psum x4, blocking collectives, on_device(): totals = lax.psum(local_total, ('row', 'col'))  148 us
    ppermute x28, waiting for transfers between devices, on_device(): lax.ppermute(ring[-1], 'col', [(dev, (dev + 1) % 8) for dev in range(8)])  128 us
    psum x1, blocking collectives, on_device(): seed_total = lax.psum(jnp.sum(seed_float, axis=1), ('row', 'col'))  42 us
    pmax x1, blocking collectives, on_device(): lax.pmax(jnp.max(jnp.abs(updated - current), axis=(0, 2)), ('row', 'col'))  41.5 us
    scatter-add x16, other arithmetic, apply_tiles(): return partial_value.at[target_block].add(product * weight[:, None, None])  35.8 us
    dot_general x16, matrix products, apply_tiles(): jnp.einsum('tkc,trc->tkr', taken_rows, panel_block, preferred_element_typ...  29.7 us
    all_to_all x3, blocking collectives, on_device(): lax.all_to_all(shaped, 'row', split_axis=0, concat_axis=0, tiled=True)  24.6 us
    convert_element_type x16, other arithmetic, advance(): weight = (begin_at + lane_index < count_here).astype(jnp.float32)  10.4 us
  transfers between devices with their start and end apart: 31, of which 27 were waited for; matrix products, arithmetic and copies ran while one was open for 7% of the time, Pallas kernels for 0%

profile of v1, /device:TPU:0, one launch (start us, length us, event | category | flops | bytes accessed | tf_op | source)
XLA Modules:
  0.0 506.3 jit_solution(15349318308590136326)
XLA Ops:
  1.6 42.0 %psum.35 = f32[8]{0:T(128)S(1)} all-reduce(f32[8]{0:T(128)S(1)} %convert_reduce_fusion.1), channel_id=1, replica_groups=mesh['row'=4,'col'=8] {'row','col'}, use_global_device_ids=true, to_apply=%region_5.6 | all-reduce | flops 8 | bytes 64 | tf_op jit(solution)/shard_map/psum | solution.py:54
  84.5 28.4 %while.44 = (s32[]{:T(128)}, f32[16,8,128]{2,1,0:T(8,128)}, s32[]{:T(128)}, s32[128]{0:T(128)S(1)}, s32[128]{0:T(128)S(1)}, /*index=5*/bf16[128,8,128]{2,1,0:T(8...) while((s32[]{:T(128)}, f32[16,8,128]{2,1,0:T(8,128)}, ...), condition=%wide.region_8.10_spmd.clone, body=%wide.region_6.9_spmd.clone.sunk | while | flops 8455462 | bytes 1774899 | solution.py:87
  121.4 36.9 %psum.36 = f32[8]{0:T(128)S(1)} all-reduce(f32[8]{0:T(128)S(1)} %get-tuple-element.491), channel_id=1, replica_groups=mesh['row'=4,'col'=8] {'row','col'}, use_global_device_ids=true, to_apply=%region_12.14 | all-reduce | flops 8 | bytes 64 | tf_op jit(solution)/shard_map/psum | solution.py:119
  163.5 5.1 %collective-permute-done.8 = bf16[16,8,128]{2,0,1:T(8,128)(2,1)S(1)} collective-permute-done((bf16[16,8,128]{2,0,1:T(8,128)(2,1)S(1)}, bf16[16,8,128]{2,0,1:T(8,128)(2,1)S(1)}, u32[]{:S(2)}, u32[]{:S(2)}) %collective-permute-start.8) | collective-permute-done | bytes 32800 | tf_op jit(solution)/shard_map/ppermute | solution.py:68
  168.6 5.1 %collective-permute-done.9 = bf16[16,8,128]{2,0,1:T(8,128)(2,1)S(1)} collective-permute-done((bf16[16,8,128]{2,0,1:T(8,128)(2,1)S(1)}, bf16[16,8,128]{2,0,1:T(8,128)(2,1)S(1)}, u32[]{:S(2)}, u32[]{:S(2)}) %collective-permute-start.9) | collective-permute-done | bytes 32800 | tf_op jit(solution)/shard_map/ppermute | solution.py:68
  173.8 5.1 %collective-permute-done.10 = bf16[16,8,128]{2,0,1:T(8,128)(2,1)S(1)} collective-permute-done((bf16[16,8,128]{2,0,1:T(8,128)(2,1)S(1)}, bf16[16,8,128]{2,0,1:T(8,128)(2,1)S(1)}, u32[]{:S(2)}, u32[]{:S(2)}) %collective-permute-start.10) | collective-permute-done | bytes 32800 | tf_op jit(solution)/shard_map/ppermute | solution.py:68
  178.9 5.1 %collective-permute-done.11 = bf16[16,8,128]{2,0,1:T(8,128)(2,1)S(1)} collective-permute-done((bf16[16,8,128]{2,0,1:T(8,128)(2,1)S(1)}, bf16[16,8,128]{2,0,1:T(8,128)(2,1)S(1)}, u32[]{:S(2)}, u32[]{:S(2)}) %collective-permute-start.11) | collective-permute-done | bytes 32800 | tf_op jit(solution)/shard_map/ppermute | solution.py:68
  184.1 5.1 %collective-permute-done.12 = bf16[16,8,128]{2,0,1:T(8,128)(2,1)S(1)} collective-permute-done((bf16[16,8,128]{2,0,1:T(8,128)(2,1)S(1)}, bf16[16,8,128]{2,0,1:T(8,128)(2,1)S(1)}, u32[]{:S(2)}, u32[]{:S(2)}) %collective-permute-start.12) | collective-permute-done | bytes 32800 | tf_op jit(solution)/shard_map/ppermute | solution.py:68
  189.2 5.1 %collective-permute-done.13 = bf16[16,8,128]{2,0,1:T(8,128)(2,1)S(1)} collective-permute-done((bf16[16,8,128]{2,0,1:T(8,128)(2,1)S(1)}, bf16[16,8,128]{2,0,1:T(8,128)(2,1)S(1)}, u32[]{:S(2)}, u32[]{:S(2)}) %collective-permute-start.13) | collective-permute-done | bytes 32800 | tf_op jit(solution)/shard_map/ppermute | solution.py:68
  194.8 19.7 %while.45 = (s32[]{:T(128)}, f32[16,8,128]{2,1,0:T(8,128)S(1)}, s32[]{:T(128)}, s32[128]{0:T(128)S(1)}, s32[128]{0:T(128)S(1)}, /*index=5*/bf16[128,8,128]{2,1,0...) while((s32[]{:T(128)}, f32[16,8,128]{2,1,0:T(8,128)S(1)}, ...), condition=%wide.region_15.17_spmd.clone, body=%wide.region_13.16_spmd.clone.sunk | while | flops 8455462 | bytes 1774899 | solution.py:87
  214.5 8.2 %all_to_all.34 = f32[4,4,8,128]{3,2,1,0:T(8,128)S(1)} all-to-all(f32[4,4,8,128]{3,2,1,0:T(8,128)S(1)} %bitcast.217), channel_id=1, replica_groups=mesh['row'=4,'col'=8] {'row'}, dimensions={0} | all-to-all | bytes 131072 | tf_op jit(solution)/shard_map/all_to_all | solution.py:110
  223.0 36.9 %psum.37 = f32[8]{0:T(128)S(1)} all-reduce(f32[8]{0:T(128)S(1)} %get-tuple-element.404), channel_id=1, replica_groups=mesh['row'=4,'col'=8] {'row','col'}, use_global_device_ids=true, to_apply=%region_17.19 | all-reduce | flops 8 | bytes 64 | tf_op jit(solution)/shard_map/psum | solution.py:119
  265.1 5.1 %collective-permute-done.15 = bf16[16,8,128]{2,0,1:T(8,128)(2,1)S(1)} collective-permute-done((bf16[16,8,128]{2,0,1:T(8,128)(2,1)S(1)}, bf16[16,8,128]{2,0,1:T(8,128)(2,1)S(1)}, u32[]{:S(2)}, u32[]{:S(2)}) %collective-permute-start.15) | collective-permute-done | bytes 32800 | tf_op jit(solution)/shard_map/ppermute | solution.py:68
  270.3 5.1 %collective-permute-done.16 = bf16[16,8,128]{2,0,1:T(8,128)(2,1)S(1)} collective-permute-done((bf16[16,8,128]{2,0,1:T(8,128)(2,1)S(1)}, bf16[16,8,128]{2,0,1:T(8,128)(2,1)S(1)}, u32[]{:S(2)}, u32[]{:S(2)}) %collective-permute-start.16) | collective-permute-done | bytes 32800 | tf_op jit(solution)/shard_map/ppermute | solution.py:68
  275.4 5.1 %collective-permute-done.17 = bf16[16,8,128]{2,0,1:T(8,128)(2,1)S(1)} collective-permute-done((bf16[16,8,128]{2,0,1:T(8,128)(2,1)S(1)}, bf16[16,8,128]{2,0,1:T(8,128)(2,1)S(1)}, u32[]{:S(2)}, u32[]{:S(2)}) %collective-permute-start.17) | collective-permute-done | bytes 32800 | tf_op jit(solution)/shard_map/ppermute | solution.py:68
  280.5 5.1 %collective-permute-done.18 = bf16[16,8,128]{2,0,1:T(8,128)(2,1)S(1)} collective-permute-done((bf16[16,8,128]{2,0,1:T(8,128)(2,1)S(1)}, bf16[16,8,128]{2,0,1:T(8,128)(2,1)S(1)}, u32[]{:S(2)}, u32[]{:S(2)}) %collective-permute-start.18) | collective-permute-done | bytes 32800 | tf_op jit(solution)/shard_map/ppermute | solution.py:68
  285.7 5.1 %collective-permute-done.19 = bf16[16,8,128]{2,0,1:T(8,128)(2,1)S(1)} collective-permute-done((bf16[16,8,128]{2,0,1:T(8,128)(2,1)S(1)}, bf16[16,8,128]{2,0,1:T(8,128)(2,1)S(1)}, u32[]{:S(2)}, u32[]{:S(2)}) %collective-permute-start.19) | collective-permute-done | bytes 32800 | tf_op jit(solution)/shard_map/ppermute | solution.py:68
  296.4 19.7 %while.46 = (s32[]{:T(128)}, f32[16,8,128]{2,1,0:T(8,128)S(1)}, s32[]{:T(128)}, s32[128]{0:T(128)S(1)}, s32[128]{0:T(128)S(1)}, /*index=5*/bf16[128,8,128]{2,1,0...) while((s32[]{:T(128)}, f32[16,8,128]{2,1,0:T(8,128)S(1)}, ...), condition=%wide.region_20.22_spmd.clone, body=%wide.region_18.21_spmd.clone.sunk | while | flops 8455462 | bytes 1774899 | solution.py:87
  316.1 8.2 %all_to_all.35 = f32[4,4,8,128]{3,2,1,0:T(8,128)S(1)} all-to-all(f32[4,4,8,128]{3,2,1,0:T(8,128)S(1)} %bitcast.218), channel_id=1, replica_groups=mesh['row'=4,'col'=8] {'row'}, dimensions={0} | all-to-all | bytes 131072 | tf_op jit(solution)/shard_map/all_to_all | solution.py:110
  324.6 37.1 %psum.38 = f32[8]{0:T(128)S(1)} all-reduce(f32[8]{0:T(128)S(1)} %get-tuple-element.406), channel_id=1, replica_groups=mesh['row'=4,'col'=8] {'row','col'}, use_global_device_ids=true, to_apply=%region_22.24 | all-reduce | flops 8 | bytes 64 | tf_op jit(solution)/shard_map/psum | solution.py:119
  398.2 19.7 %while.47 = (s32[]{:T(128)}, f32[16,8,128]{2,1,0:T(8,128)S(1)}, s32[]{:T(128)}, s32[128]{0:T(128)S(1)}, s32[128]{0:T(128)S(1)}, /*index=5*/bf16[128,8,128]{2,1,0...) while((s32[]{:T(128)}, f32[16,8,128]{2,1,0:T(8,128)S(1)}, ...), condition=%wide.region_25.27_spmd.clone, body=%wide.region_23.26_spmd.clone.sunk | while | flops 8455462 | bytes 1774899 | solution.py:87
  417.9 8.2 %all_to_all.36 = f32[4,4,8,128]{3,2,1,0:T(8,128)S(1)} all-to-all(f32[4,4,8,128]{3,2,1,0:T(8,128)S(1)} %bitcast.216), channel_id=1, replica_groups=mesh['row'=4,'col'=8] {'row'}, dimensions={0} | all-to-all | bytes 131072 | tf_op jit(solution)/shard_map/all_to_all | solution.py:110
  426.4 36.9 %psum.39 = f32[8]{0:T(128)S(1)} all-reduce(f32[8]{0:T(128)S(1)} %get-tuple-element.495), channel_id=1, replica_groups=mesh['row'=4,'col'=8] {'row','col'}, use_global_device_ids=true, to_apply=%region_27.29 | all-reduce | flops 8 | bytes 64 | tf_op jit(solution)/shard_map/psum | solution.py:119
  464.2 41.5 %all-reduce = (f32[1,8]{1,0:T(1,128)S(1)}, f32[1,8]{1,0:T(1,128)S(1)}, f32[1,8]{1,0:T(1,128)S(1)}, f32[1,8]{1,0:T(1,128)S(1)}) all-reduce(f32[1,8]{1,0:T(1,128)S(1)} %bitcast.228, f32[1,8]{1,0:T(1,128)S(1)} %bitcast.227, f32[1,8]{1,0:T(1,128)S(1)} %bitcast.230, f32[1,8]{1,0:T(1,128)S(1)} %bitcast.229), channel_id=1, replica_groups=mesh['row'=4,'col'=8] {'row','col'}, use_global_device_ids=true, to_apply=%region_35.37 | all-reduce | flops 32 | bytes 256 | tf_op jit(solution)/shard_map/pmax | solution.py:121
  (230 shorter events, 191.9 us)
Async XLA Ops:
  44.6 6.1 %collective-permute-start = (bf16[16,8,128]{2,0,1:T(8,128)(2,1)S(1)}, bf16[16,8,128]{2,0,1:T(8,128)(2,1)S(1)}, u32[]{:S(2)}, u32[]{:S(2)}) collective-permute-start(bf16[16,8,128]{2,0,1:T(8,128)(2,1)S(1)} %bitcast.225), channel_id=1, source_target_pairs={{0,1},{1,2},{2,3},{3,4},{4,5},{5,6},{6,7},{7,0},{8,9},{9,10},{10,1... | collective-permute-start | bytes 98312 | tf_op jit(solution)/shard_map/ppermute | solution.py:68
  47.1 30.9 %all-to-all-start = ((s32[4,1,4]{2,1,0:T(1,128)}), s32[4,1,4]{2,1,0:T(1,128)S(1)}, u32[]{:S(2)}, u32[]{:S(2)}) async-start(s32[4,1,4]{2,1,0:T(1,128)} %bitcast.3), calls=%async_computation | async-start | bytes 4096 | tf_op jit(solution)/shard_map/all_to_all | solution.py:96
  50.6 5.1 %collective-permute-start.1 = (bf16[16,8,128]{2,0,1:T(8,128)(2,1)S(1)}, bf16[16,8,128]{2,0,1:T(8,128)(2,1)S(1)}, u32[]{:S(2)}, u32[]{:S(2)}) collective-permute-start(bf16[16,8,128]{2,0,1:T(8,128)(2,1)S(1)} %collective-permute-done), channel_id=1, source_target_pairs={{0,1},{1,2},{2,3},{3,4},{4,5},{5,6},{6,7},{7,0},{8,9},{9,10},{10,1... | collective-permute-start | bytes 98312 | tf_op jit(solution)/shard_map/ppermute | solution.py:68
  55.8 5.1 %collective-permute-start.2 = (bf16[16,8,128]{2,0,1:T(8,128)(2,1)S(1)}, bf16[16,8,128]{2,0,1:T(8,128)(2,1)S(1)}, u32[]{:S(2)}, u32[]{:S(2)}) collective-permute-start(bf16[16,8,128]{2,0,1:T(8,128)(2,1)S(1)} %collective-permute-done.1), channel_id=1, source_target_pairs={{0,1},{1,2},{2,3},{3,4},{4,5},{5,6},{6,7},{7,0},{8,9},{9,10},{10,1... | collective-permute-start | bytes 98312 | tf_op jit(solution)/shard_map/ppermute | solution.py:68
  60.9 5.1 %collective-permute-start.3 = (bf16[16,8,128]{2,0,1:T(8,128)(2,1)S(1)}, bf16[16,8,128]{2,0,1:T(8,128)(2,1)S(1)}, u32[]{:S(2)}, u32[]{:S(2)}) collective-permute-start(bf16[16,8,128]{2,0,1:T(8,128)(2,1)S(1)} %collective-permute-done.2), channel_id=1, source_target_pairs={{0,1},{1,2},{2,3},{3,4},{4,5},{5,6},{6,7},{7,0},{8,9},{9,10},{10,1... | collective-permute-start | bytes 98312 | tf_op jit(solution)/shard_map/ppermute | solution.py:68
  66.1 5.1 %collective-permute-start.4 = (bf16[16,8,128]{2,0,1:T(8,128)(2,1)S(1)}, bf16[16,8,128]{2,0,1:T(8,128)(2,1)S(1)}, u32[]{:S(2)}, u32[]{:S(2)}) collective-permute-start(bf16[16,8,128]{2,0,1:T(8,128)(2,1)S(1)} %collective-permute-done.3), channel_id=1, source_target_pairs={{0,1},{1,2},{2,3},{3,4},{4,5},{5,6},{6,7},{7,0},{8,9},{9,10},{10,1... | collective-permute-start | bytes 98312 | tf_op jit(solution)/shard_map/ppermute | solution.py:68
  71.2 5.1 %collective-permute-start.5 = (bf16[16,8,128]{2,0,1:T(8,128)(2,1)S(1)}, bf16[16,8,128]{2,0,1:T(8,128)(2,1)S(1)}, u32[]{:S(2)}, u32[]{:S(2)}) collective-permute-start(bf16[16,8,128]{2,0,1:T(8,128)(2,1)S(1)} %collective-permute-done.4), channel_id=1, source_target_pairs={{0,1},{1,2},{2,3},{3,4},{4,5},{5,6},{6,7},{7,0},{8,9},{9,10},{10,1... | collective-permute-start | bytes 98312 | tf_op jit(solution)/shard_map/ppermute | solution.py:68
  76.3 7.1 %collective-permute-start.6 = (bf16[16,8,128]{2,0,1:T(8,128)(2,1)S(1)}, bf16[16,8,128]{2,0,1:T(8,128)(2,1)S(1)}, u32[]{:S(2)}, u32[]{:S(2)}) collective-permute-start(bf16[16,8,128]{2,0,1:T(8,128)(2,1)S(1)} %collective-permute-done.5), channel_id=1, source_target_pairs={{0,1},{1,2},{2,3},{3,4},{4,5},{5,6},{6,7},{7,0},{8,9},{9,10},{10,1... | collective-permute-start | bytes 98312 | tf_op jit(solution)/shard_map/ppermute | solution.py:68
  78.0 34.9 %all-to-all-start.2 = ((f32[4,4,1,128]{3,1,2,0:T(4,128)}), f32[4,4,1,128]{3,1,2,0:T(4,128)S(1)}, u32[]{:S(2)}, u32[]{:S(2)}) async-start(f32[4,4,1,128]{3,1,2,0:T(4,128)} %bitcast.14), calls=%async_computation.2 | async-start | bytes 16384 | tf_op jit(solution)/shard_map/all_to_all | solution.py:95
  112.9 8.1 %all-to-all-start.1 = ((f32[4,4,8,128]{3,2,1,0:T(8,128)}), f32[4,4,8,128]{3,2,1,0:T(8,128)S(1)}, u32[]{:S(2)}, u32[]{:S(2)}) async-start(f32[4,4,8,128]{3,2,1,0:T(8,128)} %bitcast.8), calls=%async_computation.1 | async-start | bytes 131072 | tf_op jit(solution)/shard_map/all_to_all | solution.py:94
  158.3 5.2 %collective-permute-start.7 = (bf16[16,8,128]{2,0,1:T(8,128)(2,1)S(1)}, bf16[16,8,128]{2,0,1:T(8,128)(2,1)S(1)}, u32[]{:S(2)}, u32[]{:S(2)}) collective-permute-start(bf16[16,8,128]{2,0,1:T(8,128)(2,1)S(1)} %get-tuple-element.481), channel_id=1, source_target_pairs={{0,1},{1,2},{2,3},{3,4},{4,5},{5,6},{6,7},{7,0},{8,9},{9,10},{10,1... | collective-permute-start | bytes 98312 | tf_op jit(solution)/shard_map/ppermute | solution.py:68
  163.5 5.1 %collective-permute-start.8 = (bf16[16,8,128]{2,0,1:T(8,128)(2,1)S(1)}, bf16[16,8,128]{2,0,1:T(8,128)(2,1)S(1)}, u32[]{:S(2)}, u32[]{:S(2)}) collective-permute-start(bf16[16,8,128]{2,0,1:T(8,128)(2,1)S(1)} %collective-permute-done.7), channel_id=1, source_target_pairs={{0,1},{1,2},{2,3},{3,4},{4,5},{5,6},{6,7},{7,0},{8,9},{9,10},{10,1... | collective-permute-start | bytes 98312 | tf_op jit(solution)/shard_map/ppermute | solution.py:68
  168.6 5.1 %collective-permute-start.9 = (bf16[16,8,128]{2,0,1:T(8,128)(2,1)S(1)}, bf16[16,8,128]{2,0,1:T(8,128)(2,1)S(1)}, u32[]{:S(2)}, u32[]{:S(2)}) collective-permute-start(bf16[16,8,128]{2,0,1:T(8,128)(2,1)S(1)} %collective-permute-done.8), channel_id=1, source_target_pairs={{0,1},{1,2},{2,3},{3,4},{4,5},{5,6},{6,7},{7,0},{8,9},{9,10},{10,1... | collective-permute-start | bytes 98312 | tf_op jit(solution)/shard_map/ppermute | solution.py:68
  173.8 5.1 %collective-permute-start.10 = (bf16[16,8,128]{2,0,1:T(8,128)(2,1)S(1)}, bf16[16,8,128]{2,0,1:T(8,128)(2,1)S(1)}, u32[]{:S(2)}, u32[]{:S(2)}) collective-permute-start(bf16[16,8,128]{2,0,1:T(8,128)(2,1)S(1)} %collective-permute-done.9), channel_id=1, source_target_pairs={{0,1},{1,2},{2,3},{3,4},{4,5},{5,6},{6,7},{7,0},{8,9},{9,10},{10,1... | collective-permute-start | bytes 98312 | tf_op jit(solution)/shard_map/ppermute | solution.py:68
  178.9 5.1 %collective-permute-start.11 = (bf16[16,8,128]{2,0,1:T(8,128)(2,1)S(1)}, bf16[16,8,128]{2,0,1:T(8,128)(2,1)S(1)}, u32[]{:S(2)}, u32[]{:S(2)}) collective-permute-start(bf16[16,8,128]{2,0,1:T(8,128)(2,1)S(1)} %collective-permute-done.10), channel_id=1, source_target_pairs={{0,1},{1,2},{2,3},{3,4},{4,5},{5,6},{6,7},{7,0},{8,9},{9,10},{10,1... | collective-permute-start | bytes 98312 | tf_op jit(solution)/shard_map/ppermute | solution.py:68
  184.1 5.1 %collective-permute-start.12 = (bf16[16,8,128]{2,0,1:T(8,128)(2,1)S(1)}, bf16[16,8,128]{2,0,1:T(8,128)(2,1)S(1)}, u32[]{:S(2)}, u32[]{:S(2)}) collective-permute-start(bf16[16,8,128]{2,0,1:T(8,128)(2,1)S(1)} %collective-permute-done.11), channel_id=1, source_target_pairs={{0,1},{1,2},{2,3},{3,4},{4,5},{5,6},{6,7},{7,0},{8,9},{9,10},{10,1... | collective-permute-start | bytes 98312 | tf_op jit(solution)/shard_map/ppermute | solution.py:68
  189.2 5.1 %collective-permute-start.13 = (bf16[16,8,128]{2,0,1:T(8,128)(2,1)S(1)}, bf16[16,8,128]{2,0,1:T(8,128)(2,1)S(1)}, u32[]{:S(2)}, u32[]{:S(2)}) collective-permute-start(bf16[16,8,128]{2,0,1:T(8,128)(2,1)S(1)} %collective-permute-done.12), channel_id=1, source_target_pairs={{0,1},{1,2},{2,3},{3,4},{4,5},{5,6},{6,7},{7,0},{8,9},{9,10},{10,1... | collective-permute-start | bytes 98312 | tf_op jit(solution)/shard_map/ppermute | solution.py:68
  259.9 5.2 %collective-permute-start.14 = (bf16[16,8,128]{2,0,1:T(8,128)(2,1)S(1)}, bf16[16,8,128]{2,0,1:T(8,128)(2,1)S(1)}, u32[]{:S(2)}, u32[]{:S(2)}) collective-permute-start(bf16[16,8,128]{2,0,1:T(8,128)(2,1)S(1)} %get-tuple-element.479), channel_id=1, source_target_pairs={{0,1},{1,2},{2,3},{3,4},{4,5},{5,6},{6,7},{7,0},{8,9},{9,10},{10,1... | collective-permute-start | bytes 98312 | tf_op jit(solution)/shard_map/ppermute | solution.py:68
  265.1 5.1 %collective-permute-start.15 = (bf16[16,8,128]{2,0,1:T(8,128)(2,1)S(1)}, bf16[16,8,128]{2,0,1:T(8,128)(2,1)S(1)}, u32[]{:S(2)}, u32[]{:S(2)}) collective-permute-start(bf16[16,8,128]{2,0,1:T(8,128)(2,1)S(1)} %collective-permute-done.14), channel_id=1, source_target_pairs={{0,1},{1,2},{2,3},{3,4},{4,5},{5,6},{6,7},{7,0},{8,9},{9,10},{10,1... | collective-permute-start | bytes 98312 | tf_op jit(solution)/shard_map/ppermute | solution.py:68
  270.3 5.1 %collective-permute-start.16 = (bf16[16,8,128]{2,0,1:T(8,128)(2,1)S(1)}, bf16[16,8,128]{2,0,1:T(8,128)(2,1)S(1)}, u32[]{:S(2)}, u32[]{:S(2)}) collective-permute-start(bf16[16,8,128]{2,0,1:T(8,128)(2,1)S(1)} %collective-permute-done.15), channel_id=1, source_target_pairs={{0,1},{1,2},{2,3},{3,4},{4,5},{5,6},{6,7},{7,0},{8,9},{9,10},{10,1... | collective-permute-start | bytes 98312 | tf_op jit(solution)/shard_map/ppermute | solution.py:68
  275.4 5.1 %collective-permute-start.17 = (bf16[16,8,128]{2,0,1:T(8,128)(2,1)S(1)}, bf16[16,8,128]{2,0,1:T(8,128)(2,1)S(1)}, u32[]{:S(2)}, u32[]{:S(2)}) collective-permute-start(bf16[16,8,128]{2,0,1:T(8,128)(2,1)S(1)} %collective-permute-done.16), channel_id=1, source_target_pairs={{0,1},{1,2},{2,3},{3,4},{4,5},{5,6},{6,7},{7,0},{8,9},{9,10},{10,1... | collective-permute-start | bytes 98312 | tf_op jit(solution)/shard_map/ppermute | solution.py:68
  280.5 5.1 %collective-permute-start.18 = (bf16[16,8,128]{2,0,1:T(8,128)(2,1)S(1)}, bf16[16,8,128]{2,0,1:T(8,128)(2,1)S(1)}, u32[]{:S(2)}, u32[]{:S(2)}) collective-permute-start(bf16[16,8,128]{2,0,1:T(8,128)(2,1)S(1)} %collective-permute-done.17), channel_id=1, source_target_pairs={{0,1},{1,2},{2,3},{3,4},{4,5},{5,6},{6,7},{7,0},{8,9},{9,10},{10,1... | collective-permute-start | bytes 98312 | tf_op jit(solution)/shard_map/ppermute | solution.py:68
  285.7 5.1 %collective-permute-start.19 = (bf16[16,8,128]{2,0,1:T(8,128)(2,1)S(1)}, bf16[16,8,128]{2,0,1:T(8,128)(2,1)S(1)}, u32[]{:S(2)}, u32[]{:S(2)}) collective-permute-start(bf16[16,8,128]{2,0,1:T(8,128)(2,1)S(1)} %collective-permute-done.18), channel_id=1, source_target_pairs={{0,1},{1,2},{2,3},{3,4},{4,5},{5,6},{6,7},{7,0},{8,9},{9,10},{10,1... | collective-permute-start | bytes 98312 | tf_op jit(solution)/shard_map/ppermute | solution.py:68
  361.7 5.2 %collective-permute-start.21 = (bf16[16,8,128]{2,0,1:T(8,128)(2,1)S(1)}, bf16[16,8,128]{2,0,1:T(8,128)(2,1)S(1)}, u32[]{:S(2)}, u32[]{:S(2)}) collective-permute-start(bf16[16,8,128]{2,0,1:T(8,128)(2,1)S(1)} %get-tuple-element.477), channel_id=1, source_target_pairs={{0,1},{1,2},{2,3},{3,4},{4,5},{5,6},{6,7},{7,0},{8,9},{9,10},{10,1... | collective-permute-start | bytes 98312 | tf_op jit(solution)/shard_map/ppermute | solution.py:68
  (9 other events, 185.3 us)
